TPU v7x, 32 devices: a whole 2x2x4 slice. The times are simulated.
32 devices in a mesh: kpt: 2 (over x), px: 16 (over z, y, core).
Axes of the slice: x: 2, y: 2, z: 4, core: 2. Of those that a mesh axis runs over, the one named last changes fastest.
Arguments:
- right_side: float32 [2, 3, 2, 64, 4096], P(None, None, 'kpt', 'px'), parts along dimension 2, may hold values from -6 to 6
- material: int32 [64, 4096], P('px'), may hold values from 0 to 2
- permittivity: float32 [3], replicated, may hold values from 1 to 2
- bloch_phase: float32 [6], P('kpt'), parts along dimension 0, may hold values from -3.140625 to 3.140625
- quad_shift: float32 [2], replicated, may hold values from 0.05 to 0.6, as said below
Outputs:
- solution: float32 [2, 3, 2, 64, 4096], P(None, None, 'kpt', 'px'), parts along dimension 2
- residual: float32 [2, 3, 2, 64, 4096], P(None, None, 'kpt', 'px'), parts along dimension 2
There are 2 independent parts, one for each index of `kpt`. A program takes and returns all parts, laid end to end along the dimension named above; an argument that names none is the same for every part. Nothing has to cross between parts.
Inputs may be any that keep to these rules, and one draw needn't show every extreme that they name: quad_shift[0] lies in 0.05 to 0.1 and quad_shift[1] in 0.3 to 0.6.
All inputs are finite; a program needn't handle non-finite values.
Results may differ from a plain program's by a relative error of at most 0.0003.
Values sent between devices are 32-bit elements; how exact they have to be, the bound alone decides.
A program may use at most 128 MiB of HBM per device.

v0:
```python
import math
import jax
import jax.numpy as jnp
from jax import lax
from jax.sharding import PartitionSpec as P

NG = 64
ITERS = 3
PRECISE = lax.Precision.HIGHEST


def from_behind(value, axis, steps):
    count = lax.axis_size(axis)
    pairs = [(source, (source + steps) % count) for source in range(count)]
    return lax.ppermute(value, axis, pairs)


def padded(shard, sides, width):
    for axis, dim in sides:
        size, length = (lax.axis_size(axis), shard.shape[dim])
        up = [(i, (i + 1) % size) for i in range(size)]
        down = [(j, i) for i, j in up]
        last = lax.slice_in_dim(shard, length - width, length, axis=dim)
        first = lax.slice_in_dim(shard, 0, width, axis=dim)
        before = lax.ppermute(last, axis, up)
        after = lax.ppermute(first, axis, down)
        shard = jnp.concatenate([before, shard, after], axis=dim)
    return shard


def block_solve(matrix_re, matrix_im, right_re, right_im):
    blocks = matrix_re.shape[0]
    system = jnp.concatenate(
        [jnp.concatenate([matrix_re, -matrix_im], 1), jnp.concatenate([matrix_im, matrix_re], 1)], 0
    )
    values = jnp.concatenate([right_re, right_im], 0)
    doubled = 2 * blocks
    pivot_row = 0
    factors = system[pivot_row + 1 :, pivot_row : pivot_row + 1] / system[pivot_row, pivot_row]
    system = jnp.concatenate(
        [
            system[: pivot_row + 1],
            system[pivot_row + 1 :] - factors * system[pivot_row : pivot_row + 1],
        ],
        0,
    )
    values = jnp.concatenate(
        [
            values[: pivot_row + 1],
            values[pivot_row + 1 :] - factors * values[pivot_row : pivot_row + 1],
        ],
        0,
    )
    rows_out = [None] * doubled
    for pivot_row in range(doubled - 1, -1, -1):
        running = values[pivot_row]
        for later_row in range(pivot_row + 1, doubled):
            running = running - system[pivot_row, later_row] * rows_out[later_row]
        rows_out[pivot_row] = running / system[pivot_row, pivot_row]
    solved = jnp.stack(rows_out, 0)
    return (solved[:blocks], solved[blocks:])


def material_scale(material, permittivity):
    scaled = jnp.zeros(material.shape, jnp.float32)
    for material_id in range(permittivity.shape[0]):
        scaled = scaled + jnp.where(
            material == material_id, permittivity[material_id], jnp.float32(0.0)
        )
    return scaled


def rotate(fields, cosine, sine_part):
    return jnp.stack(
        [cosine * fields[0] - sine_part * fields[1], sine_part * fields[0] + cosine * fields[1]]
    )


def edge_mask(fields, along, target):
    layout = tuple(
        (fields.shape[place_dim] if place_dim == along else 1 for place_dim in range(fields.ndim))
    )
    return lax.broadcasted_iota(jnp.int32, layout, along) == target


def forward_step(fields, along, cosine, sine_part):
    rolled = jnp.roll(fields, -1, along)
    return (
        jnp.where(
            edge_mask(fields, along, fields.shape[along] - 1),
            rotate(rolled, cosine, sine_part),
            rolled,
        )
        - fields
    )


def backward_step(fields, along, cosine, sine_part):
    rolled = jnp.roll(fields, 1, along)
    return (
        jnp.where(edge_mask(fields, along, 0), rotate(rolled, cosine, -sine_part), rolled) - fields
    )


def next_step(fields, upper_next):
    return jnp.concatenate([fields[:, :, 1:], upper_next], 2) - fields


def prior_step(fields, lower_prev):
    return jnp.concatenate([lower_prev, fields[:, :, :-1]], 2) - fields


def curl(fields, upper_next, turn_values):
    cosine_y, sine_y, cosine_z, sine_z = turn_values
    first = forward_step(fields[:, 2], 3, cosine_y, sine_y) - forward_step(
        fields[:, 1], 4, cosine_z, sine_z
    )
    second = forward_step(fields[:, 0], 4, cosine_z, sine_z) - next_step(
        fields[:, 2], upper_next[:, 1]
    )
    third = next_step(fields[:, 1], upper_next[:, 0]) - forward_step(
        fields[:, 0], 3, cosine_y, sine_y
    )
    return jnp.stack([first, second, third], 1)


def curl_adjoint(fields, lower_prev, turn_values):
    cosine_y, sine_y, cosine_z, sine_z = turn_values
    first = backward_step(fields[:, 1], 4, cosine_z, sine_z) - backward_step(
        fields[:, 2], 3, cosine_y, sine_y
    )
    second = prior_step(fields[:, 2], lower_prev[:, 1]) - backward_step(
        fields[:, 0], 4, cosine_z, sine_z
    )
    third = backward_step(fields[:, 0], 3, cosine_y, sine_y) - prior_step(
        fields[:, 1], lower_prev[:, 0]
    )
    return jnp.stack([first, second, third], 1)


def transform_table(theta_value, forward):
    row_index = lax.broadcasted_iota(jnp.int32, (NG, NG), 0)
    col_index = lax.broadcasted_iota(jnp.int32, (NG, NG), 1)
    angles = (
        2.0 * math.pi * (row_index * col_index % NG).astype(jnp.float32) / NG
        + theta_value * col_index.astype(jnp.float32) / NG
    )
    if forward:
        return (jnp.cos(angles), -jnp.sin(angles))
    return (jnp.cos(angles) / NG, jnp.sin(angles) / NG)


def contract(fields, tables, pattern):
    real_part = jnp.einsum(pattern, fields[0], tables[0], precision=PRECISE) - jnp.einsum(
        pattern, fields[1], tables[1], precision=PRECISE
    )
    imag_part = jnp.einsum(pattern, fields[0], tables[1], precision=PRECISE) + jnp.einsum(
        pattern, fields[1], tables[0], precision=PRECISE
    )
    return jnp.stack([real_part, imag_part])


def column_symbol(fields, bloch_phase, damping, col_start):
    length_axis = fields.shape[4]
    mode_index = lax.broadcasted_iota(jnp.int32, (NG, 1), 0).astype(jnp.float32)
    columns = col_start + lax.broadcasted_iota(jnp.int32, (1, length_axis), 1)
    kappa_x = (2.0 * math.pi * mode_index + bloch_phase[0]) / NG
    kappa_y = (2.0 * math.pi * (columns // NG).astype(jnp.float32) + bloch_phase[1]) / NG
    kappa_z = (2.0 * math.pi * (columns % NG).astype(jnp.float32) + bloch_phase[2]) / NG
    differences = [(jnp.cos(kappa) - 1.0, jnp.sin(kappa)) for kappa in (kappa_x, kappa_y, kappa_z)]
    inner_re = sum(
        (
            differences[which_one][0] * fields[0, which_one]
            + differences[which_one][1] * fields[1, which_one]
            for which_one in range(3)
        )
    )
    inner_im = sum(
        (
            differences[which_one][0] * fields[1, which_one]
            - differences[which_one][1] * fields[0, which_one]
            for which_one in range(3)
        )
    )
    magnitude = sum(
        (differences[which_one][0] ** 2 + differences[which_one][1] ** 2 for which_one in range(3))
    )
    outputs = []
    for which_one in range(3):
        diff_re, diff_im = differences[which_one]
        out_re = (fields[0, which_one] + (diff_re * inner_re - diff_im * inner_im) / damping) / (
            magnitude + damping
        )
        out_im = (fields[1, which_one] + (diff_re * inner_im + diff_im * inner_re) / damping) / (
            magnitude + damping
        )
        outputs.append(jnp.stack([out_re, out_im]))
    return jnp.stack(outputs, 1)


def gram(left_side, right_part):
    pattern = "cvxn,cwxn->vw"
    real_part = jnp.einsum(pattern, left_side[0], right_part[0], precision=PRECISE) + jnp.einsum(
        pattern, left_side[1], right_part[1], precision=PRECISE
    )
    imag_part = jnp.einsum(pattern, left_side[0], right_part[1], precision=PRECISE) - jnp.einsum(
        pattern, left_side[1], right_part[0], precision=PRECISE
    )
    return (real_part, imag_part)


def mix(fields, step_coef):
    pattern = "cvxn,vw->cwxn"
    real_part = jnp.einsum(pattern, fields[0], step_coef[0], precision=PRECISE) - jnp.einsum(
        pattern, fields[1], step_coef[1], precision=PRECISE
    )
    imag_part = jnp.einsum(pattern, fields[0], step_coef[1], precision=PRECISE) + jnp.einsum(
        pattern, fields[1], step_coef[0], precision=PRECISE
    )
    return jnp.stack([real_part, imag_part])


def on_device(right_side, material, permittivity, bloch_phase, quad_shift):
    vectors = right_side.shape[2]
    planes = right_side.shape[3]
    position = lax.axis_index("px")
    last_device = lax.axis_size("px") - 1
    permit = material_scale(material, permittivity).reshape(planes, NG, NG)
    inverse_eps = 1.0 / permit
    lower_kind = from_behind(material[-1:], "px", 1)
    inverse_lower = 1.0 / material_scale(lower_kind, permittivity).reshape(1, NG, NG)
    damping = quad_shift[0] * jnp.mean(permittivity)
    turn_values = (
        jnp.cos(bloch_phase[1]),
        jnp.sin(bloch_phase[1]),
        jnp.cos(bloch_phase[2]),
        jnp.sin(bloch_phase[2]),
    )
    is_top = position == last_device
    is_bottom = position == 0
    cosine_up = jnp.where(is_top, jnp.cos(bloch_phase[0]), 1.0)
    sine_up = jnp.where(is_top, jnp.sin(bloch_phase[0]), 0.0)
    cosine_down = jnp.where(is_bottom, jnp.cos(bloch_phase[0]), 1.0)
    sine_down = jnp.where(is_bottom, -jnp.sin(bloch_phase[0]), 0.0)
    forward_tables = [transform_table(bloch_phase[which_one], True) for which_one in range(3)]
    inverse_tables = [transform_table(bloch_phase[which_one], False) for which_one in range(3)]
    columns = NG * NG // lax.axis_size("px")
    col_start = position * columns

    def column_work(pieces):
        spectrum = contract(pieces, forward_tables[0], "cvjn,mj->cvmn")
        spectrum = column_symbol(spectrum, bloch_phase, damping, col_start)
        return contract(spectrum, inverse_tables[0], "cvmn,mj->cvjn")

    def precondition(flat_field):
        fields = flat_field.reshape(2, 3, vectors, planes, NG, NG)
        fields = contract(fields, forward_tables[2], "cvxyj,mj->cvxym")
        fields = contract(fields, forward_tables[1], "cvxjz,mj->cvxmz")
        flat_spectrum = fields.reshape(2, 3, vectors, planes, NG * NG)
        gathered = lax.all_to_all(flat_spectrum, "px", split_axis=4, concat_axis=3, tiled=True)
        worked = column_work(gathered)
        returned = lax.all_to_all(worked, "px", split_axis=3, concat_axis=4, tiled=True)
        fields = returned.reshape(2, 3, vectors, planes, NG, NG)
        fields = contract(fields, inverse_tables[1], "cvxmz,mj->cvxjz")
        fields = contract(fields, inverse_tables[2], "cvxym,mj->cvxyj")
        return fields.reshape(flat_field.shape)

    solution = jnp.zeros_like(right_side)
    residual = right_side
    direction = precondition(residual)
    for iteration in range(ITERS):
        operate_fields = direction.reshape(2, 3, direction.shape[2], planes, NG, NG)
        extended = padded(operate_fields, (("px", 3),), 1)
        bottom = rotate(extended[:, :, :, :1], cosine_down, sine_down)
        top_plane = rotate(extended[:, :, :, -1:], cosine_up, sine_up)
        extended = jnp.concatenate([bottom, extended[:, :, :, 1:-1], top_plane], 3)
        curled = curl(
            extended[:, :, :, :-1], extended[:, 1:3, :, -1:], turn_values
        ) * jnp.concatenate([inverse_lower, inverse_eps], 0)
        result = curl_adjoint(curled[:, :, :, 1:], curled[:, 1:3, :, :1], turn_values)
        mass_term = rotate(operate_fields, quad_shift[0], quad_shift[1]) * permit
        image_dir = (result + mass_term).reshape(direction.shape)
        first_pair = gram(direction, image_dir)
        second_pair = gram(direction, residual)
        totals = lax.psum((first_pair[0], first_pair[1], second_pair[0], second_pair[1]), "px")
        step_coef = block_solve(totals[0], totals[1], totals[2], totals[3])
        solution = solution + mix(direction, step_coef)
        residual = residual - mix(image_dir, step_coef)
        if iteration < ITERS - 1:
            precond = precondition(residual)
            update_pair = gram(image_dir, precond)
            update_totals = lax.psum((update_pair[0], update_pair[1]), "px")
            beta_re, beta_im = block_solve(totals[0], totals[1], update_totals[0], update_totals[1])
            direction = precond + mix(direction, (-beta_re, -beta_im))
    return (solution, residual)


def solution(mesh):
    return jax.shard_map(
        on_device,
        mesh=mesh,
        in_specs=(P(None, None, "kpt", "px", None), P("px", None), P(), P("kpt"), P()),
        out_specs=(P(None, None, "kpt", "px", None), P(None, None, "kpt", "px", None)),
        check_vma=False,
    )
```

profile of v0, /device:TPU:0, one launch (start us, length us, event | category | flops | bytes accessed | tf_op | source)
XLA Modules:
  0.0 819.2 jit_solution(17893291572140384924)
XLA Ops:
  17.2 10.4 %copy.2218 = f32[1,3,1,4,4096]{3,0,2,1,4:T(1,128)} copy(f32[1,3,1,4,4096]{4,3,1,2,0:T(4,128)S(1)} %stack.595) | data formatting | bytes 393216 | tf_op jit(solution)/shard_map/stack | solution.py:160
  27.6 10.1 %copy.2219 = f32[1,3,1,4,4096]{3,0,2,1,4:T(1,128)} copy(f32[1,3,1,4,4096]{4,3,1,2,0:T(4,128)S(1)} %stack.596) | data formatting | bytes 393216 | tf_op jit(solution)/shard_map/stack | solution.py:160
  37.7 16.6 %fusion.762 = f32[4096,3,1,2,4]{4,3,2,1,0:T(2,128)} fusion(f32[1,3,1,4,4096]{3,0,2,1,4:T(1,128)} %copy.2219, f32[1,3,1,4,4096]{3,0,2,1,4:T(1,128)} %copy.2218), kind=kLoop, calls=%fused_computation.1223 | loop fusion | flops 98304 | bytes 786432
  54.4 17.6 %reshape.14430 = f32[16,1,6144]{2,1,0:T(1,128)} reshape(f32[4096,3,1,2,4]{4,3,2,1,0:T(2,128)} %fusion.762) | data formatting | bytes 786432
  72.0 7.2 all-to-all-start
  86.4 5.0 all-to-all-done
  93.4 24.8 %reshape.14431 = f32[4096,3,1,2,4]{4,3,2,1,0:T(2,128)} reshape(f32[16,6144]{1,0:T(8,128)S(1)} %reduce.68) | data formatting | bytes 786432
  118.2 15.5 %copy.2220 = f32[2,3,1,4,16,256]{5,3,4,1,2,0:T(4,128)S(1)} copy(f32[2,3,1,4,16,256]{3,0,1,5,4,2:T(2,128)} %bitcast.1769) | data formatting | bytes 786432 | tf_op jit(solution)/shard_map/all_to_all | solution.py:260
  139.3 4.0 all-to-all-start.1
  143.3 1.9 select_add_fusion
  150.2 2.0 fusion.340
  152.4 3.0 all-to-all-done.1
  162.6 2.2 subtract_bitcast_fusion
  166.5 4.5 collective-permute-start.1
  171.2 1.5 pad_maximum_fusion.3
  189.9 1.9 fusion.47
  202.4 1.6 maximum_select_fusion.12
  212.5 32.6 %all-reduce.4 = (f32[1,1]{1,0:T(1,128)}, f32[1,1]{1,0:T(1,128)}, f32[1,1]{1,0:T(1,128)}, f32[1,1]{1,0:T(1,128)}) all-reduce(f32[1,1]{1,0:T(1,128)} %bitcast.259, f32[1,1]{1,0:T(1,128)} %bitcast.256, f32[1,1]{1,0:T(1,128)} %bitcast.260, f32[1,1]{1,0:T(1,128)} %bitcast.154), channel_id=1, replica_groups=mesh['kpt'=2,'px'=16] {'px'}, use_global_device_ids=true, to_apply=%region_3.4 | all-reduce | flops 4 | bytes 32 | tf_op jit(solution)/shard_map/psum | solution.py:285
  254.8 1.6 convolution_subtract_fusion.7
  259.9 10.4 %copy.2320 = f32[1,3,1,4,4096]{3,0,2,1,4:T(1,128)} copy(f32[1,3,1,4,4096]{4,3,1,2,0:T(4,128)S(1)} %stack.650) | data formatting | bytes 393216 | tf_op jit(solution)/shard_map/stack | solution.py:160
  270.3 10.1 %copy.2321 = f32[1,3,1,4,4096]{3,0,2,1,4:T(1,128)} copy(f32[1,3,1,4,4096]{4,3,1,2,0:T(4,128)S(1)} %stack.651) | data formatting | bytes 393216 | tf_op jit(solution)/shard_map/stack | solution.py:160
  280.5 16.6 %fusion.761 = f32[4096,3,1,2,4]{4,3,2,1,0:T(2,128)} fusion(f32[1,3,1,4,4096]{3,0,2,1,4:T(1,128)} %copy.2321, f32[1,3,1,4,4096]{3,0,2,1,4:T(1,128)} %copy.2320), kind=kLoop, calls=%fused_computation.1222 | loop fusion | flops 98304 | bytes 786432
  297.1 17.0 %reshape.14432 = f32[16,1,6144]{2,1,0:T(1,128)S(1)} reshape(f32[4096,3,1,2,4]{4,3,2,1,0:T(2,128)} %fusion.761) | data formatting | bytes 786432
  314.1 15.2 %all_to_all.90 = f32[16,1,6144]{2,1,0:T(1,128)S(1)} all-to-all(f32[16,1,6144]{2,1,0:T(1,128)S(1)} %reshape.14432), channel_id=1, replica_groups=mesh['kpt'=2,'px'=16] {'px'}, dimensions={0} | all-to-all | bytes 786432 | tf_op jit(solution)/shard_map/all_to_all | solution.py:260
  329.2 1.5 reduce.69
  330.7 24.8 %reshape.14433 = f32[4096,3,1,2,4]{4,3,2,1,0:T(2,128)} reshape(f32[16,6144]{1,0:T(8,128)S(1)} %reduce.69) | data formatting | bytes 786432
  355.5 15.5 %copy.2322 = f32[2,3,1,4,16,256]{5,3,4,1,2,0:T(4,128)S(1)} copy(f32[2,3,1,4,16,256]{3,0,1,5,4,2:T(2,128)} %bitcast.1770) | data formatting | bytes 786432 | tf_op jit(solution)/shard_map/all_to_all | solution.py:260
  375.9 15.5 %all_to_all.91 = f32[2,3,1,64,256]{4,0,2,1,3:T(2,128)S(1)} all-to-all(f32[2,3,1,64,256]{4,0,2,1,3:T(2,128)S(1)} %copy.2339), channel_id=1, replica_groups=mesh['kpt'=2,'px'=16] {'px'}, dimensions={3} | all-to-all | bytes 786432 | tf_op jit(solution)/shard_map/all_to_all | solution.py:262
  401.8 33.2 %all-reduce.3 = (f32[1,1]{1,0:T(1,128)}, f32[1,1]{1,0:T(1,128)}) all-reduce(f32[1,1]{1,0:T(1,128)} %bitcast.335, f32[1,1]{1,0:T(1,128)} %bitcast.334), channel_id=1, replica_groups=mesh['kpt'=2,'px'=16] {'px'}, use_global_device_ids=true, to_apply=%region_6.7 | all-reduce | flops 2 | bytes 16 | tf_op jit(solution)/shard_map/psum | solution.py:292
  444.4 4.6 collective-permute-start.4
  465.8 1.7 copy.2379
  467.5 1.7 copy.2370
  495.1 32.3 %all-reduce.2 = (f32[1,1]{1,0:T(1,128)}, f32[1,1]{1,0:T(1,128)}, f32[1,1]{1,0:T(1,128)}, f32[1,1]{1,0:T(1,128)}) all-reduce(f32[1,1]{1,0:T(1,128)} %bitcast.436, f32[1,1]{1,0:T(1,128)} %bitcast.431, f32[1,1]{1,0:T(1,128)} %bitcast.439, f32[1,1]{1,0:T(1,128)} %bitcast.348), channel_id=1, replica_groups=mesh['kpt'=2,'px'=16] {'px'}, use_global_device_ids=true, to_apply=%region_9.10 | all-reduce | flops 4 | bytes 32 | tf_op jit(solution)/shard_map/psum | solution.py:285
  541.3 10.4 %copy.2435 = f32[1,3,1,4,4096]{3,0,2,1,4:T(1,128)} copy(f32[1,3,1,4,4096]{4,3,1,2,0:T(4,128)S(1)} %stack.714) | data formatting | bytes 393216 | tf_op jit(solution)/shard_map/stack | solution.py:160
  551.7 10.1 %copy.2436 = f32[1,3,1,4,4096]{3,0,2,1,4:T(1,128)} copy(f32[1,3,1,4,4096]{4,3,1,2,0:T(4,128)S(1)} %stack.715) | data formatting | bytes 393216 | tf_op jit(solution)/shard_map/stack | solution.py:160
  561.8 16.6 %fusion.760 = f32[4096,3,1,2,4]{4,3,2,1,0:T(2,128)} fusion(f32[1,3,1,4,4096]{3,0,2,1,4:T(1,128)} %copy.2436, f32[1,3,1,4,4096]{3,0,2,1,4:T(1,128)} %copy.2435), kind=kLoop, calls=%fused_computation.1221 | loop fusion | flops 98304 | bytes 786432
  578.5 17.0 %reshape.14434 = f32[16,1,6144]{2,1,0:T(1,128)S(1)} reshape(f32[4096,3,1,2,4]{4,3,2,1,0:T(2,128)} %fusion.760) | data formatting | bytes 786432
  595.4 14.9 %all_to_all.92 = f32[16,1,6144]{2,1,0:T(1,128)S(1)} all-to-all(f32[16,1,6144]{2,1,0:T(1,128)S(1)} %reshape.14434), channel_id=1, replica_groups=mesh['kpt'=2,'px'=16] {'px'}, dimensions={0} | all-to-all | bytes 786432 | tf_op jit(solution)/shard_map/all_to_all | solution.py:260
  610.4 1.5 reduce.70
  611.9 24.8 %reshape.14435 = f32[4096,3,1,2,4]{4,3,2,1,0:T(2,128)} reshape(f32[16,6144]{1,0:T(8,128)S(1)} %reduce.70) | data formatting | bytes 786432
  636.7 15.5 %copy.2437 = f32[2,3,1,4,16,256]{5,3,4,1,2,0:T(4,128)S(1)} copy(f32[2,3,1,4,16,256]{3,0,1,5,4,2:T(2,128)} %bitcast.1771) | data formatting | bytes 786432 | tf_op jit(solution)/shard_map/all_to_all | solution.py:260
  657.1 15.5 %all_to_all.93 = f32[2,3,1,64,256]{4,0,2,1,3:T(2,128)S(1)} all-to-all(f32[2,3,1,64,256]{4,0,2,1,3:T(2,128)S(1)} %copy.2442), channel_id=1, replica_groups=mesh['kpt'=2,'px'=16] {'px'}, dimensions={3} | all-to-all | bytes 786432 | tf_op jit(solution)/shard_map/all_to_all | solution.py:262
  682.4 33.4 %all-reduce.1 = (f32[1,1]{1,0:T(1,128)}, f32[1,1]{1,0:T(1,128)}) all-reduce(f32[1,1]{1,0:T(1,128)} %bitcast.501, f32[1,1]{1,0:T(1,128)} %bitcast.500), channel_id=1, replica_groups=mesh['kpt'=2,'px'=16] {'px'}, use_global_device_ids=true, to_apply=%region_12.13 | all-reduce | flops 2 | bytes 16 | tf_op jit(solution)/shard_map/psum | solution.py:292
  727.9 4.6 collective-permute-start.6
  743.7 1.6 maximum_select_fusion.8
  751.4 2.4 fusion.56
  766.8 1.9 fusion.85
  777.2 32.3 %all-reduce = (f32[1,1]{1,0:T(1,128)}, f32[1,1]{1,0:T(1,128)}, f32[1,1]{1,0:T(1,128)}, f32[1,1]{1,0:T(1,128)}) all-reduce(f32[1,1]{1,0:T(1,128)} %bitcast.589, f32[1,1]{1,0:T(1,128)} %bitcast.584, f32[1,1]{1,0:T(1,128)} %bitcast.592, f32[1,1]{1,0:T(1,128)} %bitcast.514), channel_id=1, replica_groups=mesh['kpt'=2,'px'=16] {'px'}, use_global_device_ids=true, to_apply=%region_15.16 | all-reduce | flops 4 | bytes 32 | tf_op jit(solution)/shard_map/psum | solution.py:285
  (717 shorter events, 200.9 us)
Async XLA Ops:
  1.5 148.7 %collective-permute-start.2 = (s32[1,4096]{1,0:T(1,128)S(1)}, s32[1,4096]{1,0:T(1,128)S(1)}, u32[]{:S(2)}, u32[]{:S(2)}) collective-permute-start(s32[1,4096]{1,0:T(1,128)S(1)} %slice.1041), channel_id=1, source_target_pairs={{0,1},{1,2},{2,3},{3,4},{4,5},{5,6},{6,7},{7,8},{8,9},{9,10},{10,1... | collective-permute-start | bytes 49160 | tf_op jit(solution)/shard_map/ppermute | solution.py:15
  4.1 393.6 %copy-start.96 = (f32[64]{0:T(128)}, f32[64]{0:T(128)S(1)}, u32[]{:S(2)}) copy-start(f32[64]{0:T(128)S(1)} %multiply_multiply_fusion) | copy-start | bytes 772
  8.6 386.4 %copy-start.98 = (f32[64]{0:T(128)}, f32[64]{0:T(128)S(1)}, u32[]{:S(2)}) copy-start(f32[64]{0:T(128)S(1)} %multiply_multiply_fusion.2) | copy-start | bytes 772
  54.4 24.9 %copy-start.136 = (f32[3]{0:T(128)S(1)}, f32[3]{0:T(128)}, u32[]{:S(2)}) copy-start(f32[3]{0:T(128)} %param.7) | copy-start | bytes 40
  54.4 26.0 %copy-start.137 = (f32[2]{0:T(128)S(1)}, f32[2]{0:T(128)}, u32[]{:S(2)}) copy-start(f32[2]{0:T(128)} %param.9) | copy-start | bytes 28
  72.0 19.4 %all-to-all-start = ((f32[16,1,6144]{2,1,0:T(1,128)}), f32[16,1,6144]{2,1,0:T(1,128)S(1)}, u32[]{:S(2)}, u32[]{:S(2)}) async-start(f32[16,1,6144]{2,1,0:T(1,128)} %reshape.14430), calls=%async_computation | async-start | bytes 786432 | tf_op jit(solution)/shard_map/all_to_all | solution.py:260
  82.3 53.7 %copy-start.126 = (f32[64]{0:T(128)}, f32[64]{0:T(128)S(1)}, u32[]{:S(2)}) copy-start(f32[64]{0:T(128)S(1)} %get-tuple-element.318) | copy-start | bytes 772
  82.3 53.7 %copy-start.129 = (f32[64]{0:T(128)}, f32[64]{0:T(128)S(1)}, u32[]{:S(2)}) copy-start(f32[64]{0:T(128)S(1)} %get-tuple-element.319) | copy-start | bytes 772
  83.0 53.0 %copy-start.132 = (f32[64]{0:T(128)}, f32[64]{0:T(128)S(1)}, u32[]{:S(2)}) copy-start(f32[64]{0:T(128)S(1)} %get-tuple-element.321) | copy-start | bytes 772
  83.0 292.1 %copy-start.100 = (f32[64]{0:T(128)}, f32[64]{0:T(128)S(1)}, u32[]{:S(2)}) copy-start(f32[64]{0:T(128)S(1)} %get-tuple-element.320) | copy-start | bytes 772
  84.3 288.9 %copy-start.109 = (f32[256]{0:T(256)}, f32[256]{0:T(256)S(1)}, u32[]{:S(2)}) copy-start(f32[256]{0:T(256)S(1)} %get-tuple-element.323) | copy-start | bytes 3076
  84.3 288.9 %copy-start.111 = (f32[256]{0:T(256)}, f32[256]{0:T(256)S(1)}, u32[]{:S(2)}) copy-start(f32[256]{0:T(256)S(1)} %get-tuple-element.322) | copy-start | bytes 3076
  85.0 288.2 %copy-start.113 = (f32[256]{0:T(256)}, f32[256]{0:T(256)S(1)}, u32[]{:S(2)}) copy-start(f32[256]{0:T(256)S(1)} %get-tuple-element.314) | copy-start | bytes 3076
  85.0 288.2 %copy-start.115 = (f32[256]{0:T(256)}, f32[256]{0:T(256)S(1)}, u32[]{:S(2)}) copy-start(f32[256]{0:T(256)S(1)} %get-tuple-element.315) | copy-start | bytes 3076
  85.7 287.6 %copy-start.117 = (f32[256]{0:T(256)}, f32[256]{0:T(256)S(1)}, u32[]{:S(2)}) copy-start(f32[256]{0:T(256)S(1)} %get-tuple-element.316) | copy-start | bytes 3076
  85.7 287.6 %copy-start.119 = (f32[256]{0:T(256)}, f32[256]{0:T(256)S(1)}, u32[]{:S(2)}) copy-start(f32[256]{0:T(256)S(1)} %get-tuple-element.317) | copy-start | bytes 3076
  137.7 5.6 copy-start.108
  139.3 16.1 %all-to-all-start.1 = ((f32[2,3,1,64,256]{4,0,2,1,3:T(2,128)}), f32[2,3,1,64,256]{4,0,2,1,3:T(2,128)S(1)}, u32[]{:S(2)}, u32[]{:S(2)}) async-start(f32[2,3,1,64,256]{4,0,2,1,3:T(2,128)} %copy.2232), calls=%async_computation.1 | async-start | bytes 786432 | tf_op jit(solution)/shard_map/all_to_all | solution.py:262
  145.4 59.1 %copy-start.20 = (f32[4,64,64]{2,1,0:T(8,128)}, f32[4,64,64]{2,1,0:T(8,128)S(1)}, u32[]{:S(2)}) copy-start(f32[4,64,64]{2,1,0:T(8,128)S(1)} %reshape.14242) | copy-start | bytes 196612
  146.0 43.9 %copy-start.123 = (pred[64]{0:T(512)(128)(4,1)}, pred[64]{0:T(512)(128)(4,1)S(1)}, u32[]{:S(2)}) copy-start(pred[64]{0:T(512)(128)(4,1)S(1)} %iota_compare_fusion) | copy-start | bytes 196
  152.4 321.9 %copy-start.14 = (f32[5,64,64]{2,0,1:T(8,128)}, f32[5,64,64]{2,0,1:T(8,128)S(1)}, u32[]{:S(2)}) copy-start(f32[5,64,64]{2,0,1:T(8,128)S(1)} %copy.2823) | copy-start | bytes 245764
  161.5 5.0 copy-start.22
  162.5 8.5 %collective-permute-start = (f32[2,3,1,1,64,64]{5,3,4,2,1,0:T(1,128)S(1)}, f32[2,3,1,1,64,64]{5,3,4,2,1,0:T(1,128)S(1)}, u32[]{:S(2)}, u32[]{:S(2)}) collective-permute-start(f32[2,3,1,1,64,64]{5,3,4,2,1,0:T(1,128)S(1)} %get-tuple-element.141), channel_id=1, source_target_pairs={{0,1},{1,2},{2,3},{3,4},{4,5},{5,6},{6,7},{7,8},{8,9},{9,10},{10,1... | collective-permute-start | bytes 294920 | tf_op jit(solution)/shard_map/ppermute | solution.py:25
  166.5 22.2 %collective-permute-start.1 = (f32[2,3,1,1,64,64]{5,3,4,2,1,0:T(1,128)}, f32[2,3,1,1,64,64]{5,3,4,2,1,0:T(1,128)}, u32[]{:S(2)}, u32[]{:S(2)}) collective-permute-start(f32[2,3,1,1,64,64]{5,3,4,2,1,0:T(1,128)} %get-tuple-element.142), channel_id=1, source_target_pairs={{1,0},{2,1},{3,2},{4,3},{5,4},{6,5},{7,6},{8,7},{9,8},{10,9},{11,1... | collective-permute-start | bytes 294920 | tf_op jit(solution)/shard_map/ppermute | solution.py:26
  187.0 2.9 copy-start.33
  188.7 283.9 %copy-start.54 = (f32[1,3,1,1,64,64]{5,4,3,2,1,0:T(8,128)}, f32[1,3,1,1,64,64]{5,4,3,2,1,0:T(8,128)S(1)}, u32[]{:S(2)}) copy-start(f32[1,3,1,1,64,64]{5,4,3,2,1,0:T(8,128)S(1)} %mul.3410) | copy-start | bytes 147460
  398.3 41.0 %copy-start.43 = (f32[3,4,4096]{2,1,0:T(4,128)S(1)}, f32[3,4,4096]{2,1,0:T(4,128)}, u32[]{:S(2)}) copy-start(f32[3,4,4096]{2,1,0:T(4,128)} %reshape.14240) | copy-start | bytes 589828
  441.9 7.1 copy-start.88
  441.9 7.1 copy-start.89
  444.4 8.0 collective-permute-start.3
  444.4 28.2 %collective-permute-start.4 = (f32[2,3,1,1,64,64]{5,3,4,2,1,0:T(1,128)}, f32[2,3,1,1,64,64]{5,3,4,2,1,0:T(1,128)}, u32[]{:S(2)}, u32[]{:S(2)}) collective-permute-start(f32[2,3,1,1,64,64]{5,3,4,2,1,0:T(1,128)} %get-tuple-element.136), channel_id=1, source_target_pairs={{1,0},{2,1},{3,2},{4,3},{5,4},{6,5},{7,6},{8,7},{9,8},{10,9},{11,1... | collective-permute-start | bytes 294920 | tf_op jit(solution)/shard_map/ppermute | solution.py:26
  449.0 3.4 copy-start.57
  453.1 2.8 copy-start.3
  462.8 2.8 copy-start.106
  487.7 47.1 %copy-start.24 = (f32[1,3,1,4,4096]{4,3,1,2,0:T(4,128)S(1)}, f32[1,3,1,4,4096]{4,3,1,2,0:T(4,128)}, u32[]{:S(2)}) copy-start(f32[1,3,1,4,4096]{4,3,1,2,0:T(4,128)} %copy-done.23) | copy-start | bytes 589828
  487.7 47.1 %copy-start.27 = (f32[1,3,1,4,4096]{4,3,1,2,0:T(4,128)S(1)}, f32[1,3,1,4,4096]{4,3,1,2,0:T(4,128)}, u32[]{:S(2)}) copy-start(f32[1,3,1,4,4096]{4,3,1,2,0:T(4,128)} %copy-done.26) | copy-start | bytes 589828
  636.7 15.7 %copy-start.101 = (f32[64]{0:T(128)S(1)}, f32[64]{0:T(128)}, u32[]{:S(2)}) copy-start(f32[64]{0:T(128)} %copy-done.100) | copy-start | bytes 772
  723.6 8.9 %collective-permute-start.5 = (f32[2,3,1,1,64,64]{5,3,4,2,1,0:T(1,128)S(1)}, f32[2,3,1,1,64,64]{5,3,4,2,1,0:T(1,128)S(1)}, u32[]{:S(2)}, u32[]{:S(2)}) collective-permute-start(f32[2,3,1,1,64,64]{5,3,4,2,1,0:T(1,128)S(1)} %copy.2808), channel_id=1, source_target_pairs={{0,1},{1,2},{2,3},{3,4},{4,5},{5,6},{6,7},{7,8},{8,9},{9,10},{10,1... | collective-permute-start | bytes 294920 | tf_op jit(solution)/shard_map/ppermute | solution.py:25
  723.7 8.8 %copy-start.58 = (f32[1,3,1,1,64,64]{5,4,3,2,1,0:T(8,128)S(1)}, f32[1,3,1,1,64,64]{5,4,3,2,1,0:T(8,128)}, u32[]{:S(2)}) copy-start(f32[1,3,1,1,64,64]{5,4,3,2,1,0:T(8,128)} %copy-done.56) | copy-start | bytes 147460
  727.9 22.4 %collective-permute-start.6 = (f32[2,3,1,1,64,64]{5,3,0,4,2,1:T(1,128)}, f32[2,3,1,1,64,64]{5,3,0,4,2,1:T(1,128)}, u32[]{:S(2)}, u32[]{:S(2)}) collective-permute-start(f32[2,3,1,1,64,64]{5,3,0,4,2,1:T(1,128)} %get-tuple-element.131), channel_id=1, source_target_pairs={{1,0},{2,1},{3,2},{4,3},{5,4},{6,5},{7,6},{8,7},{9,8},{10,9},{11,1... | collective-permute-start | bytes 294920 | tf_op jit(solution)/shard_map/ppermute | solution.py:26
  736.2 2.9 copy-start.9
  746.3 4.0 copy-start.55
  747.0 4.4 copy-start.10
  762.7 3.3 copy-start.62
  770.4 46.4 %copy-start.25 = (f32[1,3,1,4,4096]{4,3,1,2,0:T(4,128)S(1)}, f32[1,3,1,4,4096]{4,3,1,2,0:T(4,128)}, u32[]{:S(2)}) copy-start(f32[1,3,1,4,4096]{4,3,1,2,0:T(4,128)} %copy-done.23) | copy-start | bytes 589828
  770.4 46.4 %copy-start.28 = (f32[1,3,1,4,4096]{4,3,1,2,0:T(4,128)S(1)}, f32[1,3,1,4,4096]{4,3,1,2,0:T(4,128)}, u32[]{:S(2)}) copy-start(f32[1,3,1,4,4096]{4,3,1,2,0:T(4,128)} %copy-done.26) | copy-start | bytes 589828
  770.4 46.4 %copy-start.45 = (f32[1,3,1,4,4096]{4,3,1,2,0:T(4,128)S(1)}, f32[1,3,1,4,4096]{4,3,1,2,0:T(4,128)}, u32[]{:S(2)}) copy-start(f32[1,3,1,4,4096]{4,3,1,2,0:T(4,128)} %copy-done.44) | copy-start | bytes 589828
  770.4 46.4 %copy-start.47 = (f32[1,3,1,4,4096]{4,3,1,2,0:T(4,128)S(1)}, f32[1,3,1,4,4096]{4,3,1,2,0:T(4,128)}, u32[]{:S(2)}) copy-start(f32[1,3,1,4,4096]{4,3,1,2,0:T(4,128)} %copy-done.46) | copy-start | bytes 589828
  (99 other events, 160.8 us)
where the time goes:
time: 831 us; the launch traced here: 819 us
  local copies, waits for them, and re-layouts  320 us (39%)
  blocking collectives  225 us (27%)
  other arithmetic  140 us (17%)
  between operations  51.9 us (6%)
  matrix products  48.9 us (6%)
  starting transfers between devices  25.6 us (3%)
    unnamed x312, local copies, waits for them, and re-layouts  143 us
    psum x3, blocking collectives, on_device(): lax.psum((first_pair[0], first_pair[1], second_pair[0], second_pair[1]),...  97.3 us
    another operation x20, local copies, waits for them, and re-layouts, contract(): return jnp.stack([real_part, imag_part])  67.3 us
    psum x2, blocking collectives, on_device(): update_totals = lax.psum((update_pair[0], update_pair[1]), 'px')  66.5 us
    unnamed x5, other arithmetic  51.8 us
    all_to_all x4, local copies, waits for them, and re-layouts, precondition(): lax.all_to_all(flat_spectrum, 'px', split_axis=4, concat_axis=3, tiled=True)  46.9 us
    all_to_all x2, blocking collectives, precondition(): lax.all_to_all(worked, 'px', split_axis=3, concat_axis=4, tiled=True)  31 us
    all_to_all x2, blocking collectives, precondition(): lax.all_to_all(flat_spectrum, 'px', split_axis=4, concat_axis=3, tiled=True)  30.1 us
  transfers between devices with their start and end apart: 9, of which 2 were waited for; matrix products, arithmetic and copies ran while one was open for 23% of the time, Pallas kernels for 0%

commit v1 on v0

--- a/solution.py
+++ b/solution.py
@@ -257,7 +257,9 @@
         fields = contract(fields, forward_tables[2], "cvxyj,mj->cvxym")
         fields = contract(fields, forward_tables[1], "cvxjz,mj->cvxmz")
         flat_spectrum = fields.reshape(2, 3, vectors, planes, NG * NG)
-        gathered = lax.all_to_all(flat_spectrum, "px", split_axis=4, concat_axis=3, tiled=True)
+        shards = jnp.split(flat_spectrum, lax.axis_size("px"), axis=4)
+        received = lax.all_to_all(jnp.stack(shards), "px", 0, 0)
+        gathered = jnp.concatenate(received, axis=3)
         worked = column_work(gathered)
         returned = lax.all_to_all(worked, "px", split_axis=3, concat_axis=4, tiled=True)
         fields = returned.reshape(2, 3, vectors, planes, NG, NG)

time: 831 us -> 547 us (0.66)
  local copies, waits for them, and re-layouts: 320 us -> 96.1 us
  other arithmetic: 140 us -> 83.3 us
    unnamed x312 -> x370, local copies, waits for them, and re-layouts: 143 us -> 28.7 us
    another operation x20 -> x17, local copies, waits for them, and re-layouts: 67.3 us -> 5.87 us  [contract(): return jnp.stack([real_part, imag_part])]
    unnamed x5 -> x2, other arithmetic: 51.8 us -> 1.94 us
    all_to_all x4 -> x0, local copies, waits for them, and re-layouts: 46.9 us -> none  [precondition(): lax.all_to_all(flat_spectrum, 'px', split_axis=4, concat_axis=3, tiled=True)]
  transfers between devices with their start and end apart: 9 -> 9, of which waited for: 2 -> 2; matrix products, arithmetic and copies ran while one was open for 23% -> 19% of each run, Pallas kernels for 0% -> 0%
where the time goes in v1:
time: 547 us; the launch traced here: 537 us
  blocking collectives  224 us (41%)
  local copies, waits for them, and re-layouts  96.1 us (18%)
  other arithmetic  83.3 us (15%)
  between operations  53.2 us (10%)
  matrix products  47.1 us (9%)
  starting transfers between devices  25.9 us (5%)
  waiting for transfers between devices  7.59 us (1%)
    psum x3, blocking collectives, on_device(): lax.psum((first_pair[0], first_pair[1], second_pair[0], second_pair[1]),...  96.7 us
    psum x2, blocking collectives, on_device(): update_totals = lax.psum((update_pair[0], update_pair[1]), 'px')  66.4 us
    all_to_all x2, blocking collectives, precondition(): lax.all_to_all(worked, 'px', split_axis=3, concat_axis=4, tiled=True)  31.1 us
    another operation x46, other arithmetic, rotate(): jnp.stack([cosine * fields[0] - sine_part * fields[1], sine_part * fields...  29.8 us
    all_to_all x2, blocking collectives, precondition(): received = lax.all_to_all(jnp.stack(shards), 'px', 0, 0)  29.6 us
    unnamed x370, local copies, waits for them, and re-layouts  28.7 us
    ppermute x3, starting transfers between devices, padded(): after = lax.ppermute(first, axis, down)  14.2 us
    concatenate x19, local copies, waits for them, and re-layouts, forward_step(): rolled = jnp.roll(fields, -1, along)  12.3 us
  transfers between devices with their start and end apart: 9, of which 2 were waited for; matrix products, arithmetic and copies ran while one was open for 19% of the time, Pallas kernels for 0%

profile of v1, /device:TPU:0, one launch (start us, length us, event | category | flops | bytes accessed | tf_op | source)
XLA Modules:
  0.0 536.8 jit_solution(8331032072989929378)
XLA Ops:
  2.0 1.4 fusion.759
  5.4 1.3 fusion.283
  6.7 1.3 fusion.275
  9.0 1.3 fusion.13
  10.3 1.3 fusion.265
  11.6 1.3 fusion.257
  13.0 1.3 fusion.12
  14.3 1.3 fusion.11
  15.6 1.3 fusion.10
  27.2 7.2 %all-to-all-start = ((f32[16,2,3,1,4,256]{5,4,2,1,3,0:T(4,128)}), f32[16,2,3,1,4,256]{5,4,2,1,3,0:T(4,128)S(1)}, u32[]{:S(2)}, u32[]{:S(2)}) async-start(f32[16,2,3,1,4,256]{5,4,2,1,3,0:T(4,128)} %constant_dynamic-update-slice_fusion.2), calls=%async_computation | async-start | bytes 786432 | tf_op jit(solution)/shard_map/all_to_all | solution.py:261
  38.3 1.4 fusion.398
  41.8 4.8 all-to-all-done
  52.3 3.8 all-to-all-start.1
  56.1 1.9 select_add_fusion
  63.2 2.0 fusion.340
  65.4 2.8 all-to-all-done.1
  75.4 2.2 subtract_bitcast_fusion
  78.7 4.7 collective-permute-start.1
  98.6 1.4 subtract_bitcast_fusion.5
  101.2 1.9 fusion.47
  113.7 1.6 maximum_select_fusion.12
  123.7 32.4 %all-reduce.4 = (f32[1,1]{1,0:T(1,128)}, f32[1,1]{1,0:T(1,128)}, f32[1,1]{1,0:T(1,128)}, f32[1,1]{1,0:T(1,128)}) all-reduce(f32[1,1]{1,0:T(1,128)} %bitcast.289, f32[1,1]{1,0:T(1,128)} %bitcast.286, f32[1,1]{1,0:T(1,128)} %bitcast.290, f32[1,1]{1,0:T(1,128)} %bitcast.184), channel_id=1, replica_groups=mesh['kpt'=2,'px'=16] {'px'}, use_global_device_ids=true, to_apply=%region_3.4 | all-reduce | flops 4 | bytes 32 | tf_op jit(solution)/shard_map/psum | solution.py:287
  158.7 1.4 maximum_subtract_fusion.9
  170.4 14.8 %all_to_all.60 = f32[16,2,3,1,4,256]{5,4,2,1,3,0:T(4,128)S(1)} all-to-all(f32[16,2,3,1,4,256]{5,4,2,1,3,0:T(4,128)S(1)} %constant_dynamic-update-slice_fusion.20), channel_id=1, replica_groups=mesh['kpt'=2,'px'=16] {'px'}, dimensions={0} | all-to-all | bytes 786432 | tf_op jit(solution)/shard_map/all_to_all | solution.py:261
  190.2 15.5 %all_to_all.61 = f32[2,3,1,64,256]{4,0,2,1,3:T(2,128)S(1)} all-to-all(f32[2,3,1,64,256]{4,0,2,1,3:T(2,128)S(1)} %copy.2311), channel_id=1, replica_groups=mesh['kpt'=2,'px'=16] {'px'}, dimensions={3} | all-to-all | bytes 786432 | tf_op jit(solution)/shard_map/all_to_all | solution.py:264
  216.0 33.2 %all-reduce.3 = (f32[1,1]{1,0:T(1,128)}, f32[1,1]{1,0:T(1,128)}) all-reduce(f32[1,1]{1,0:T(1,128)} %bitcast.395, f32[1,1]{1,0:T(1,128)} %bitcast.394), channel_id=1, replica_groups=mesh['kpt'=2,'px'=16] {'px'}, use_global_device_ids=true, to_apply=%region_6.7 | all-reduce | flops 2 | bytes 16 | tf_op jit(solution)/shard_map/psum | solution.py:294
  256.9 4.8 collective-permute-start.4
  261.9 1.3 multiply_subtract_fusion.1
  277.0 1.7 copy.2351
  278.7 1.7 copy.2342
  280.5 1.4 subtract_bitcast_fusion.4
  297.0 1.3 maximum_select_fusion.16
  298.4 1.3 maximum_select_fusion.15
  308.5 32.2 %all-reduce.2 = (f32[1,1]{1,0:T(1,128)}, f32[1,1]{1,0:T(1,128)}, f32[1,1]{1,0:T(1,128)}, f32[1,1]{1,0:T(1,128)}) all-reduce(f32[1,1]{1,0:T(1,128)} %bitcast.496, f32[1,1]{1,0:T(1,128)} %bitcast.491, f32[1,1]{1,0:T(1,128)} %bitcast.499, f32[1,1]{1,0:T(1,128)} %bitcast.408), channel_id=1, replica_groups=mesh['kpt'=2,'px'=16] {'px'}, use_global_device_ids=true, to_apply=%region_9.10 | all-reduce | flops 4 | bytes 32 | tf_op jit(solution)/shard_map/psum | solution.py:287
  343.3 1.4 maximum_subtract_fusion.10
  355.3 14.8 %all_to_all.62 = f32[16,2,3,1,4,256]{5,4,2,1,3,0:T(4,128)S(1)} all-to-all(f32[16,2,3,1,4,256]{5,4,2,1,3,0:T(4,128)S(1)} %constant_dynamic-update-slice_fusion.38), channel_id=1, replica_groups=mesh['kpt'=2,'px'=16] {'px'}, dimensions={0} | all-to-all | bytes 786432 | tf_op jit(solution)/shard_map/all_to_all | solution.py:261
  375.1 15.5 %all_to_all.63 = f32[2,3,1,64,256]{4,0,2,1,3:T(2,128)S(1)} all-to-all(f32[2,3,1,64,256]{4,0,2,1,3:T(2,128)S(1)} %copy.2428), channel_id=1, replica_groups=mesh['kpt'=2,'px'=16] {'px'}, dimensions={3} | all-to-all | bytes 786432 | tf_op jit(solution)/shard_map/all_to_all | solution.py:264
  397.6 1.8 multiply_reduce_fusion.2
  402.0 33.2 %all-reduce.1 = (f32[1,1]{1,0:T(1,128)}, f32[1,1]{1,0:T(1,128)}) all-reduce(f32[1,1]{1,0:T(1,128)} %bitcast.591, f32[1,1]{1,0:T(1,128)} %bitcast.590), channel_id=1, replica_groups=mesh['kpt'=2,'px'=16] {'px'}, use_global_device_ids=true, to_apply=%region_12.13 | all-reduce | flops 2 | bytes 16 | tf_op jit(solution)/shard_map/psum | solution.py:294
  444.0 1.3 multiply_subtract_fusion
  447.4 4.6 collective-permute-start.6
  452.2 1.3 fusion.29
  461.2 1.3 subtract_bitcast_fusion.2
  463.9 1.6 maximum_select_fusion.8
  467.3 1.9 copy.2970
  471.5 2.3 fusion.56
  494.8 32.2 %all-reduce = (f32[1,1]{1,0:T(1,128)}, f32[1,1]{1,0:T(1,128)}, f32[1,1]{1,0:T(1,128)}, f32[1,1]{1,0:T(1,128)}) all-reduce(f32[1,1]{1,0:T(1,128)} %bitcast.679, f32[1,1]{1,0:T(1,128)} %bitcast.674, f32[1,1]{1,0:T(1,128)} %bitcast.682, f32[1,1]{1,0:T(1,128)} %bitcast.604), channel_id=1, replica_groups=mesh['kpt'=2,'px'=16] {'px'}, use_global_device_ids=true, to_apply=%region_15.16 | all-reduce | flops 4 | bytes 32 | tf_op jit(solution)/shard_map/psum | solution.py:287
  529.5 1.3 maximum_subtract_fusion.11
  (771 shorter events, 178.6 us)
Async XLA Ops:
  1.5 61.7 %collective-permute-start.2 = (s32[1,4096]{1,0:T(1,128)S(1)}, s32[1,4096]{1,0:T(1,128)S(1)}, u32[]{:S(2)}, u32[]{:S(2)}) collective-permute-start(s32[1,4096]{1,0:T(1,128)S(1)} %slice.1041), channel_id=1, source_target_pairs={{0,1},{1,2},{2,3},{3,4},{4,5},{5,6},{6,7},{7,8},{8,9},{9,10},{10,1... | collective-permute-start | bytes 49160 | tf_op jit(solution)/shard_map/ppermute | solution.py:15
  4.1 207.8 %copy-start.95 = (f32[64]{0:T(128)}, f32[64]{0:T(128)S(1)}, u32[]{:S(2)}) copy-start(f32[64]{0:T(128)S(1)} %multiply_multiply_fusion) | copy-start | bytes 772
  8.7 200.6 %copy-start.97 = (f32[64]{0:T(128)}, f32[64]{0:T(128)S(1)}, u32[]{:S(2)}) copy-start(f32[64]{0:T(128)S(1)} %multiply_multiply_fusion.2) | copy-start | bytes 772
  17.1 17.3 %copy-start.144 = (f32[3]{0:T(128)S(1)}, f32[3]{0:T(128)}, u32[]{:S(2)}) copy-start(f32[3]{0:T(128)} %param.7) | copy-start | bytes 40
  17.1 18.5 %copy-start.145 = (f32[2]{0:T(128)S(1)}, f32[2]{0:T(128)}, u32[]{:S(2)}) copy-start(f32[2]{0:T(128)} %param.9) | copy-start | bytes 28
  27.2 19.4 %all-to-all-start = ((f32[16,2,3,1,4,256]{5,4,2,1,3,0:T(4,128)}), f32[16,2,3,1,4,256]{5,4,2,1,3,0:T(4,128)S(1)}, u32[]{:S(2)}, u32[]{:S(2)}) async-start(f32[16,2,3,1,4,256]{5,4,2,1,3,0:T(4,128)} %constant_dynamic-update-slice_fusion.2), calls=%async_computation | async-start | bytes 786432 | tf_op jit(solution)/shard_map/all_to_all | solution.py:261
  37.6 11.3 %copy-start.134 = (f32[64]{0:T(128)}, f32[64]{0:T(128)S(1)}, u32[]{:S(2)}) copy-start(f32[64]{0:T(128)S(1)} %get-tuple-element.316) | copy-start | bytes 772
  37.6 11.3 %copy-start.137 = (f32[64]{0:T(128)}, f32[64]{0:T(128)S(1)}, u32[]{:S(2)}) copy-start(f32[64]{0:T(128)S(1)} %get-tuple-element.317) | copy-start | bytes 772
  38.3 10.6 %copy-start.140 = (f32[64]{0:T(128)}, f32[64]{0:T(128)S(1)}, u32[]{:S(2)}) copy-start(f32[64]{0:T(128)S(1)} %get-tuple-element.319) | copy-start | bytes 772
  38.3 151.0 %copy-start.99 = (f32[64]{0:T(128)}, f32[64]{0:T(128)S(1)}, u32[]{:S(2)}) copy-start(f32[64]{0:T(128)S(1)} %get-tuple-element.318) | copy-start | bytes 772
  39.7 9.3 %copy-start.112 = (f32[256]{0:T(256)}, f32[256]{0:T(256)S(1)}, u32[]{:S(2)}) copy-start(f32[256]{0:T(256)S(1)} %get-tuple-element.320) | copy-start | bytes 3076
  39.7 147.9 %copy-start.110 = (f32[256]{0:T(256)}, f32[256]{0:T(256)S(1)}, u32[]{:S(2)}) copy-start(f32[256]{0:T(256)S(1)} %get-tuple-element.321) | copy-start | bytes 3076
  40.4 8.6 %copy-start.115 = (f32[256]{0:T(256)}, f32[256]{0:T(256)S(1)}, u32[]{:S(2)}) copy-start(f32[256]{0:T(256)S(1)} %get-tuple-element.312) | copy-start | bytes 3076
  40.4 8.6 %copy-start.118 = (f32[256]{0:T(256)}, f32[256]{0:T(256)S(1)}, u32[]{:S(2)}) copy-start(f32[256]{0:T(256)S(1)} %get-tuple-element.313) | copy-start | bytes 3076
  41.1 7.9 %copy-start.121 = (f32[256]{0:T(256)}, f32[256]{0:T(256)S(1)}, u32[]{:S(2)}) copy-start(f32[256]{0:T(256)S(1)} %get-tuple-element.314) | copy-start | bytes 3076
  41.1 7.9 %copy-start.124 = (f32[256]{0:T(256)}, f32[256]{0:T(256)S(1)}, u32[]{:S(2)}) copy-start(f32[256]{0:T(256)S(1)} %get-tuple-element.315) | copy-start | bytes 3076
  50.7 5.4 %copy-start.109 = (s32[4,4096]{1,0:T(4,128)S(1)}, s32[4,4096]{1,0:T(4,128)}, u32[]{:S(2)}) copy-start(s32[4,4096]{1,0:T(4,128)} %param.6) | copy-start | bytes 196612
  52.3 15.9 %all-to-all-start.1 = ((f32[2,3,1,64,256]{4,0,2,1,3:T(2,128)}), f32[2,3,1,64,256]{4,0,2,1,3:T(2,128)S(1)}, u32[]{:S(2)}, u32[]{:S(2)}) async-start(f32[2,3,1,64,256]{4,0,2,1,3:T(2,128)} %copy.2190), calls=%async_computation.1 | async-start | bytes 786432 | tf_op jit(solution)/shard_map/all_to_all | solution.py:264
  58.2 57.5 %copy-start.20 = (f32[4,64,64]{2,1,0:T(8,128)}, f32[4,64,64]{2,1,0:T(8,128)S(1)}, u32[]{:S(2)}) copy-start(f32[4,64,64]{2,1,0:T(8,128)S(1)} %reshape.14255) | copy-start | bytes 196612
  58.9 42.3 %copy-start.131 = (pred[64]{0:T(512)(128)(4,1)}, pred[64]{0:T(512)(128)(4,1)S(1)}, u32[]{:S(2)}) copy-start(pred[64]{0:T(512)(128)(4,1)S(1)} %iota_compare_fusion) | copy-start | bytes 196
  65.4 220.5 %copy-start.14 = (f32[5,64,64]{2,0,1:T(8,128)}, f32[5,64,64]{2,0,1:T(8,128)S(1)}, u32[]{:S(2)}) copy-start(f32[5,64,64]{2,0,1:T(8,128)S(1)} %copy.2809) | copy-start | bytes 245764
  75.3 8.1 %collective-permute-start = (f32[2,3,1,1,64,64]{5,3,4,2,1,0:T(1,128)S(1)}, f32[2,3,1,1,64,64]{5,3,4,2,1,0:T(1,128)S(1)}, u32[]{:S(2)}, u32[]{:S(2)}) collective-permute-start(f32[2,3,1,1,64,64]{5,3,4,2,1,0:T(1,128)S(1)} %get-tuple-element.139), channel_id=1, source_target_pairs={{0,1},{1,2},{2,3},{3,4},{4,5},{5,6},{6,7},{7,8},{8,9},{9,10},{10,1... | collective-permute-start | bytes 294920 | tf_op jit(solution)/shard_map/ppermute | solution.py:25
  78.7 21.3 %collective-permute-start.1 = (f32[2,3,1,1,64,64]{5,3,4,2,1,0:T(1,128)}, f32[2,3,1,1,64,64]{5,3,4,2,1,0:T(1,128)}, u32[]{:S(2)}, u32[]{:S(2)}) collective-permute-start(f32[2,3,1,1,64,64]{5,3,4,2,1,0:T(1,128)} %get-tuple-element.140), channel_id=1, source_target_pairs={{1,0},{2,1},{3,2},{4,3},{5,4},{6,5},{7,6},{8,7},{9,8},{10,9},{11,1... | collective-permute-start | bytes 294920 | tf_op jit(solution)/shard_map/ppermute | solution.py:26
  98.3 2.9 copy-start.32
  100.0 3.1 copy-start.51
  255.5 6.2 %copy-start.85 = (f32[1,3,1,4,4096]{4,3,1,2,0:T(4,128)S(1)}, f32[1,3,1,4,4096]{4,3,1,2,0:T(4,128)}, u32[]{:S(2)}) copy-start(f32[1,3,1,4,4096]{4,3,1,2,0:T(4,128)} %stack.852) | copy-start | bytes 589828
  255.6 6.2 %copy-start.86 = (f32[1,3,1,4,4096]{4,3,1,2,0:T(4,128)S(1)}, f32[1,3,1,4,4096]{4,3,1,2,0:T(4,128)}, u32[]{:S(2)}) copy-start(f32[1,3,1,4,4096]{4,3,1,2,0:T(4,128)} %stack.853) | copy-start | bytes 589828
  256.9 8.3 %collective-permute-start.3 = (f32[2,3,1,1,64,64]{5,3,4,2,1,0:T(1,128)S(1)}, f32[2,3,1,1,64,64]{5,3,4,2,1,0:T(1,128)S(1)}, u32[]{:S(2)}, u32[]{:S(2)}) collective-permute-start(f32[2,3,1,1,64,64]{5,3,4,2,1,0:T(1,128)S(1)} %get-tuple-element.133), channel_id=1, source_target_pairs={{0,1},{1,2},{2,3},{3,4},{4,5},{5,6},{6,7},{7,8},{8,9},{9,10},{10,1... | collective-permute-start | bytes 294920 | tf_op jit(solution)/shard_map/ppermute | solution.py:25
  256.9 26.9 %collective-permute-start.4 = (f32[2,3,1,1,64,64]{5,3,4,2,1,0:T(1,128)}, f32[2,3,1,1,64,64]{5,3,4,2,1,0:T(1,128)}, u32[]{:S(2)}, u32[]{:S(2)}) collective-permute-start(f32[2,3,1,1,64,64]{5,3,4,2,1,0:T(1,128)} %get-tuple-element.134), channel_id=1, source_target_pairs={{1,0},{2,1},{3,2},{4,3},{5,4},{6,5},{7,6},{8,7},{9,8},{10,9},{11,1... | collective-permute-start | bytes 294920 | tf_op jit(solution)/shard_map/ppermute | solution.py:26
  261.8 3.5 copy-start.55
  297.0 2.8 copy-start.81
  297.0 2.8 copy-start.83
  297.0 2.8 copy-start.89
  297.0 2.8 copy-start.90
  297.0 2.8 copy-start.102
  297.0 2.8 copy-start.103
  301.2 46.8 %copy-start.23 = (f32[1,3,1,4,4096]{4,3,1,2,0:T(4,128)S(1)}, f32[1,3,1,4,4096]{4,3,1,2,0:T(4,128)}, u32[]{:S(2)}) copy-start(f32[1,3,1,4,4096]{4,3,1,2,0:T(4,128)} %copy-done.22) | copy-start | bytes 589828
  301.3 46.8 %copy-start.26 = (f32[1,3,1,4,4096]{4,3,1,2,0:T(4,128)S(1)}, f32[1,3,1,4,4096]{4,3,1,2,0:T(4,128)}, u32[]{:S(2)}) copy-start(f32[1,3,1,4,4096]{4,3,1,2,0:T(4,128)} %copy-done.25) | copy-start | bytes 589828
  355.0 15.3 %copy-start.100 = (f32[64]{0:T(128)S(1)}, f32[64]{0:T(128)}, u32[]{:S(2)}) copy-start(f32[64]{0:T(128)} %copy-done.99) | copy-start | bytes 772
  443.0 9.0 %collective-permute-start.5 = (f32[2,3,1,1,64,64]{5,3,4,2,1,0:T(1,128)S(1)}, f32[2,3,1,1,64,64]{5,3,4,2,1,0:T(1,128)S(1)}, u32[]{:S(2)}, u32[]{:S(2)}) collective-permute-start(f32[2,3,1,1,64,64]{5,3,4,2,1,0:T(1,128)S(1)} %copy.2794), channel_id=1, source_target_pairs={{0,1},{1,2},{2,3},{3,4},{4,5},{5,6},{6,7},{7,8},{8,9},{9,10},{10,1... | collective-permute-start | bytes 294920 | tf_op jit(solution)/shard_map/ppermute | solution.py:25
  447.4 23.0 %collective-permute-start.6 = (f32[2,3,1,1,64,64]{5,3,0,4,2,1:T(1,128)}, f32[2,3,1,1,64,64]{5,3,0,4,2,1:T(1,128)}, u32[]{:S(2)}, u32[]{:S(2)}) collective-permute-start(f32[2,3,1,1,64,64]{5,3,0,4,2,1:T(1,128)} %get-tuple-element.129), channel_id=1, source_target_pairs={{1,0},{2,1},{3,2},{4,3},{5,4},{6,5},{7,6},{8,7},{9,8},{10,9},{11,1... | collective-permute-start | bytes 294920 | tf_op jit(solution)/shard_map/ppermute | solution.py:26
  456.3 2.9 copy-start.9
  467.1 3.2 copy-start.53
  467.2 4.4 copy-start.10
  487.8 46.6 %copy-start.24 = (f32[1,3,1,4,4096]{4,3,1,2,0:T(4,128)S(1)}, f32[1,3,1,4,4096]{4,3,1,2,0:T(4,128)}, u32[]{:S(2)}) copy-start(f32[1,3,1,4,4096]{4,3,1,2,0:T(4,128)} %copy-done.22) | copy-start | bytes 589828
  487.8 46.6 %copy-start.27 = (f32[1,3,1,4,4096]{4,3,1,2,0:T(4,128)S(1)}, f32[1,3,1,4,4096]{4,3,1,2,0:T(4,128)}, u32[]{:S(2)}) copy-start(f32[1,3,1,4,4096]{4,3,1,2,0:T(4,128)} %copy-done.25) | copy-start | bytes 589828
  487.8 46.6 %copy-start.42 = (f32[1,3,1,4,4096]{4,3,1,2,0:T(4,128)S(1)}, f32[1,3,1,4,4096]{4,3,1,2,0:T(4,128)}, u32[]{:S(2)}) copy-start(f32[1,3,1,4,4096]{4,3,1,2,0:T(4,128)} %copy-done.41) | copy-start | bytes 589828
  487.8 46.6 %copy-start.44 = (f32[1,3,1,4,4096]{4,3,1,2,0:T(4,128)S(1)}, f32[1,3,1,4,4096]{4,3,1,2,0:T(4,128)}, u32[]{:S(2)}) copy-start(f32[1,3,1,4,4096]{4,3,1,2,0:T(4,128)} %copy-done.43) | copy-start | bytes 589828
  (107 other events, 168.0 us)
